TPU v7x, 32 devices: a whole 2x2x4 slice. The times are simulated.
32 devices in a mesh: row: 4 (over z), col: 8 (over y, x, core).
Axes of the slice: x: 2, y: 2, z: 4, core: 2. Of those that a mesh axis runs over, the one named last changes fastest.
Arguments:
- tile_data: bfloat16 [8, 4, 8, 2, 128, 128], P(None, 'row', 'col'), may hold values from 0 to 1, as said below
- tile_cols: int32 [8, 4, 8, 2], P(None, 'row', 'col'), may hold values from -1 to 31, as said below
Outputs:
- vertex_triangles: float32 [8, 4, 128], P(None, 'row', 'col')
- triangles: float32 [], replicated
Inputs may be any that keep to these rules, and one draw needn't show every extreme that they name: `tile_cols`: slot (a, r, c, s) holds -1 (empty) or a tile column J with J % 8 == c and J >= a 4 + r; the columns of one tile row are distinct; every slot of tile row 0 is filled; tile row I keeps each slot that has an allowed column with probability (32 - I) / 32, so rows with a lower index hold more tiles on average. `tile_data`: entries are 0 or 1; tiles of empty slots are zero; a tile whose column equals its tile row is strictly upper triangular; about one entry in 8 of a stored tile is 1, with edges clustered among groups of vertices.
All inputs are finite; a program needn't handle non-finite values.
Results may differ from a plain program's by a relative error of at most 0.0003.
Values may be sent and summed in bfloat16 or wider, within the bound.
A program may use at most 128 MiB of HBM per device.

v0:
```python
import jax
import jax.numpy as jnp
from jax import lax
from jax.sharding import PartitionSpec as P

vertex_scale = 2.0 ** (-14)
total_scale = 2.0 ** (-12)


def taken_in(share, axis, dim):

    def gathered(part):
        return lax.all_gather(part, axis, axis=dim, tiled=True)

    return jax.tree.map(gathered, share)


def tile_counts(stored, middle, own_tiles, own_cols, col_tiles, col_index):
    valid = middle >= 0
    clipped = jnp.clip(middle, 0, col_tiles.shape[0] - 1).astype(jnp.int32)
    partner = col_tiles[clipped]
    partner_cols = col_index[clipped]
    matches = partner_cols[:, :, None] == own_cols[None, None, :]
    matches = matches & valid[:, None, None] & (own_cols >= 0)[None, None, :]
    weights = matches.astype(jnp.bfloat16)
    targets = jnp.einsum("pqs,sxz->pqxz", weights, own_tiles, preferred_element_type=jnp.float32)
    paths = jnp.einsum("pxy,pqyz->pqxz", stored, partner, preferred_element_type=jnp.float32)
    return jnp.sum(paths * targets, axis=(0, 1, 3))


def on_device(tile_data, tile_cols):
    rows_here = tile_data.shape[0]
    slots = tile_data.shape[3]
    width = tile_data.shape[4]
    own_tiles = tile_data[:, 0, 0]
    own_cols = tile_cols[:, 0, 0]
    row_index = lax.all_gather(tile_cols, "col", axis=2, tiled=True)
    col_index = lax.all_gather(tile_cols, "row", axis=1, tiled=True)
    col_tiles = lax.all_gather(tile_data, "row", axis=1, tiled=True)
    tile_rows = col_index.shape[0] * col_index.shape[1]
    col_index = col_index.reshape(tile_rows, slots)
    col_tiles = col_tiles.reshape(tile_rows, slots, width, width)

    def add_piece(carry, piece, start):
        devices_here = piece.shape[2]
        middle = lax.dynamic_slice_in_dim(row_index, start.astype(jnp.int32), devices_here, 2)
        middle = middle.reshape(rows_here, devices_here * slots)
        stored = piece.reshape(rows_here, devices_here * slots, width, width)

        def per_row(packed):
            return tile_counts(packed[0], packed[1], packed[2], packed[3], col_tiles, col_index)

        return carry + lax.map(per_row, (stored, middle, own_tiles, own_cols))

    initial = jnp.zeros((rows_here, width), jnp.float32)
    partial_value = add_piece(initial, taken_in(tile_data, "col", 2), jnp.int32(0))
    shares = lax.psum_scatter(
        partial_value.reshape(rows_here, 1, width), "col", scatter_dimension=2, tiled=True
    )
    vertices = tile_rows * width
    overall = lax.psum(jnp.sum(partial_value), ("row", "col"))
    return (shares * vertex_scale, overall * (total_scale / vertices))


def solution(mesh):
    return jax.shard_map(
        on_device,
        mesh=mesh,
        in_specs=(P(None, "row", "col", None, None, None), P(None, "row", "col", None)),
        out_specs=(P(None, "row", "col"), P()),
        check_vma=False,
    )
```

profile of v0, /device:TPU:0, one launch (start us, length us, event | category | flops | bytes accessed | tf_op | source)
XLA Modules:
  0.0 213.6 jit_solution(9713125407251959521)
XLA Ops:
  7.2 0.7 all-gather.3.cloned.1.call-update
  8.0 0.7 all-gather.5.cloned.1.call-update
  8.7 2.4 %copy.37 = bf16[8,1,1,2,128,128]{5,3,4,0,2,1:T(2,128)(2,1)} copy(bf16[8,1,1,2,128,128]{5,4,3,2,1,0:T(8,128)(2,1)} %param.4) | data formatting | bytes 1048576 | tf_op args[0]
  11.1 12.6 %all_gather.15 = s32[8,4,1,2]{0,3,2,1:T(2,128)S(1)} all-gather(s32[8,1,1,2]{0,3,2,1:T(2,128)S(1)} %copy-done.1), channel_id=1, replica_groups=mesh['row'=4,'col'=8] {'row'}, dimensions={1}, use_global_device_ids=true | all-gather | bytes 320 | tf_op jit(solution)/shard_map/all_gather | solution.py:38
  23.9 8.9 %all_gather.12 = s32[8,1,8,2]{0,3,1,2:T(2,128)S(1)} all-gather(s32[8,1,1,2]{0,3,1,2:T(2,128)S(1)} %bitcast.68), channel_id=1, replica_groups=mesh['row'=4,'col'=8] {'col'}, dimensions={2}, use_global_device_ids=true | all-gather | bytes 576 | tf_op jit(solution)/shard_map/all_gather | solution.py:37
  33.0 25.0 %all-gather.3.cloned.1.call-done = bf16[8,4,1,2,128,128]{5,4,3,2,1,0:T(8,128)(2,1)} async-done(((bf16[8,1,1,2,128,128]{5,4,3,2,1,0:T(8,128)(2,1)}), bf16[8,4,1,2,128,128]{5,4,3,2,1,0:T(8,128)(2,1)}) %all-gather.3.cloned.1.call-update) | async-done | bytes 2097168 | tf_op jit(solution)/shard_map/all_gather | solution.py:39
  58.0 37.3 %all-gather.5.cloned.1.call-done = bf16[8,1,8,2,128,128]{5,4,3,2,1,0:T(8,128)(2,1)} async-done(((bf16[8,1,1,2,128,128]{5,4,3,2,1,0:T(8,128)(2,1)}), bf16[8,1,8,2,128,128]{5,4,3,2,1,0:T(8,128)(2,1)}) %all-gather.5.cloned.1.call-update) | async-done | bytes 4194320 | tf_op jit(solution)/shard_map/all_gather | solution.py:13
  95.3 67.3 %while.10 = (s32[]{:T(128)}, f32[8,128]{1,0:T(8,128)S(1)}, s32[8,16]{1,0:T(8,128)S(1)}, bf16[32,2,128,128]{3,2,1,0:T(8,128)(2,1)}, bf16[8,16,128,128]{3,2,1,0:T(...) while((s32[]{:T(128)}, f32[8,128]{1,0:T(8,128)S(1)}, ...), condition=%wide.region_2.3_spmd, body=%wide.region_0.2_spmd.sunk | while | flops 137364624 | bytes 20520652 | solution.py:53
  95.3 0.6 gather_fusion
  96.0 1.4 fusion.32
  97.4 1.8 copy.41
  99.3 2.5 %gather_fusion.1 = bf16[16,2,128,128]{3,2,1,0:T(8,128)(2,1)S(1)} fusion(bf16[32,2,128,128]{3,2,1,0:T(8,128)(2,1)} %get-tuple-element.163, s32[1024]{0:T(1024)S(1)} %pad_clamp_fusion.2), kind=kCustom, calls=%fused_computation.clone.1 | custom fusion | bytes 2097216 | tf_op jit(solution)/shard_map/while/body/eval_jaxpr/gather | solution.py:21
  101.8 1.9 fusion.33
  103.7 0.6 gather_fusion
  104.4 1.4 fusion.32
  105.8 1.8 copy.41
  107.7 2.5 %gather_fusion.1 = bf16[16,2,128,128]{3,2,1,0:T(8,128)(2,1)S(1)} fusion(bf16[32,2,128,128]{3,2,1,0:T(8,128)(2,1)} %get-tuple-element.163, s32[1024]{0:T(1024)S(1)} %pad_clamp_fusion.2), kind=kCustom, calls=%fused_computation.clone.1 | custom fusion | bytes 2097216 | tf_op jit(solution)/shard_map/while/body/eval_jaxpr/gather | solution.py:21
  110.2 1.9 fusion.33
  112.1 0.6 gather_fusion
  112.8 1.4 fusion.32
  114.3 1.8 copy.41
  116.1 2.5 %gather_fusion.1 = bf16[16,2,128,128]{3,2,1,0:T(8,128)(2,1)S(1)} fusion(bf16[32,2,128,128]{3,2,1,0:T(8,128)(2,1)} %get-tuple-element.163, s32[1024]{0:T(1024)S(1)} %pad_clamp_fusion.2), kind=kCustom, calls=%fused_computation.clone.1 | custom fusion | bytes 2097216 | tf_op jit(solution)/shard_map/while/body/eval_jaxpr/gather | solution.py:21
  118.6 1.9 fusion.33
  121.2 1.4 fusion.32
  122.7 1.8 copy.41
  124.5 2.5 %gather_fusion.1 = bf16[16,2,128,128]{3,2,1,0:T(8,128)(2,1)S(1)} fusion(bf16[32,2,128,128]{3,2,1,0:T(8,128)(2,1)} %get-tuple-element.163, s32[1024]{0:T(1024)S(1)} %pad_clamp_fusion.2), kind=kCustom, calls=%fused_computation.clone.1 | custom fusion | bytes 2097216 | tf_op jit(solution)/shard_map/while/body/eval_jaxpr/gather | solution.py:21
  127.0 1.9 fusion.33
  129.6 1.4 fusion.32
  131.1 1.8 copy.41
  132.9 2.5 %gather_fusion.1 = bf16[16,2,128,128]{3,2,1,0:T(8,128)(2,1)S(1)} fusion(bf16[32,2,128,128]{3,2,1,0:T(8,128)(2,1)} %get-tuple-element.163, s32[1024]{0:T(1024)S(1)} %pad_clamp_fusion.2), kind=kCustom, calls=%fused_computation.clone.1 | custom fusion | bytes 2097216 | tf_op jit(solution)/shard_map/while/body/eval_jaxpr/gather | solution.py:21
  135.4 1.9 fusion.33
  138.0 1.4 fusion.32
  139.5 1.8 copy.41
  141.3 2.5 %gather_fusion.1 = bf16[16,2,128,128]{3,2,1,0:T(8,128)(2,1)S(1)} fusion(bf16[32,2,128,128]{3,2,1,0:T(8,128)(2,1)} %get-tuple-element.163, s32[1024]{0:T(1024)S(1)} %pad_clamp_fusion.2), kind=kCustom, calls=%fused_computation.clone.1 | custom fusion | bytes 2097216 | tf_op jit(solution)/shard_map/while/body/eval_jaxpr/gather | solution.py:21
  143.8 1.9 fusion.33
  146.4 1.4 fusion.32
  147.9 1.8 copy.41
  149.7 2.5 %gather_fusion.1 = bf16[16,2,128,128]{3,2,1,0:T(8,128)(2,1)S(1)} fusion(bf16[32,2,128,128]{3,2,1,0:T(8,128)(2,1)} %get-tuple-element.163, s32[1024]{0:T(1024)S(1)} %pad_clamp_fusion.2), kind=kCustom, calls=%fused_computation.clone.1 | custom fusion | bytes 2097216 | tf_op jit(solution)/shard_map/while/body/eval_jaxpr/gather | solution.py:21
  152.2 1.9 fusion.33
  154.9 1.4 fusion.32
  156.3 1.8 copy.41
  158.2 2.5 %gather_fusion.1 = bf16[16,2,128,128]{3,2,1,0:T(8,128)(2,1)S(1)} fusion(bf16[32,2,128,128]{3,2,1,0:T(8,128)(2,1)} %get-tuple-element.163, s32[1024]{0:T(1024)S(1)} %pad_clamp_fusion.2), kind=kCustom, calls=%fused_computation.clone.1 | custom fusion | bytes 2097216 | tf_op jit(solution)/shard_map/while/body/eval_jaxpr/gather | solution.py:21
  160.7 1.9 fusion.33
  162.8 0.8 bitcast_reduce_fusion
  163.7 0.6 reduce_sum.18
  164.3 39.5 %psum.7 = f32[]{:T(128)} all-reduce(f32[]{:T(128)} %reduce_sum.18), channel_id=1, replica_groups=mesh['row'=4,'col'=8] {'row','col'}, use_global_device_ids=true, to_apply=%region_5.6 | all-reduce | flops 1 | bytes 8 | tf_op jit(solution)/shard_map/psum | solution.py:61
  204.4 0.8 reshape_bitcast_fusion
  205.3 0.6 broadcast_multiply_fusion
  (82 shorter events, 4.9 us)
Async XLA Ops:
  7.2 4.0 %copy-start.1 = (s32[8,1,1,2]{0,3,2,1:T(2,128)S(1)}, s32[8,1,1,2]{0,3,2,1:T(2,128)}, u32[]{:S(2)}) copy-start(s32[8,1,1,2]{0,3,2,1:T(2,128)} %param.5) | copy-start | bytes 196
  7.2 50.8 %all-gather.3.cloned.1.call-start = ((), (), s32[]{:S(2)}) async-start(), calls=%async_computation.1 | async-start | bytes 2621440 | tf_op jit(solution)/shard_map/all_gather | solution.py:39
  7.9 87.4 %all-gather.5.cloned.1.call-start = ((), (), s32[]{:S(2)}) async-start(), calls=%async_computation.2 | async-start | bytes 4718592 | tf_op jit(solution)/shard_map/all_gather | solution.py:13
  8.7 195.8 %reduce-scatter.4.cloned.1.call-start = ((), (), s32[]{:S(2)}) async-start(), calls=%async_computation.3 | async-start | bytes 73728
  99.3 2.5 %copy-start = (f32[16,2,128,128]{2,3,1,0:T(8,128)S(1)}, f32[16,2,128,128]{2,3,1,0:T(8,128)}, u32[]{:S(2)}) copy-start(f32[16,2,128,128]{2,3,1,0:T(8,128)} %copy.41) | copy-start | bytes 6291460 | tf_op jit(solution)/shard_map/while
  107.7 2.5 %copy-start = (f32[16,2,128,128]{2,3,1,0:T(8,128)S(1)}, f32[16,2,128,128]{2,3,1,0:T(8,128)}, u32[]{:S(2)}) copy-start(f32[16,2,128,128]{2,3,1,0:T(8,128)} %copy.41) | copy-start | bytes 6291460 | tf_op jit(solution)/shard_map/while
  116.1 2.5 %copy-start = (f32[16,2,128,128]{2,3,1,0:T(8,128)S(1)}, f32[16,2,128,128]{2,3,1,0:T(8,128)}, u32[]{:S(2)}) copy-start(f32[16,2,128,128]{2,3,1,0:T(8,128)} %copy.41) | copy-start | bytes 6291460 | tf_op jit(solution)/shard_map/while
  124.5 2.5 %copy-start = (f32[16,2,128,128]{2,3,1,0:T(8,128)S(1)}, f32[16,2,128,128]{2,3,1,0:T(8,128)}, u32[]{:S(2)}) copy-start(f32[16,2,128,128]{2,3,1,0:T(8,128)} %copy.41) | copy-start | bytes 6291460 | tf_op jit(solution)/shard_map/while
  132.9 2.5 %copy-start = (f32[16,2,128,128]{2,3,1,0:T(8,128)S(1)}, f32[16,2,128,128]{2,3,1,0:T(8,128)}, u32[]{:S(2)}) copy-start(f32[16,2,128,128]{2,3,1,0:T(8,128)} %copy.41) | copy-start | bytes 6291460 | tf_op jit(solution)/shard_map/while
  141.3 2.5 %copy-start = (f32[16,2,128,128]{2,3,1,0:T(8,128)S(1)}, f32[16,2,128,128]{2,3,1,0:T(8,128)}, u32[]{:S(2)}) copy-start(f32[16,2,128,128]{2,3,1,0:T(8,128)} %copy.41) | copy-start | bytes 6291460 | tf_op jit(solution)/shard_map/while
  149.7 2.5 %copy-start = (f32[16,2,128,128]{2,3,1,0:T(8,128)S(1)}, f32[16,2,128,128]{2,3,1,0:T(8,128)}, u32[]{:S(2)}) copy-start(f32[16,2,128,128]{2,3,1,0:T(8,128)} %copy.41) | copy-start | bytes 6291460 | tf_op jit(solution)/shard_map/while
  158.2 2.5 %copy-start = (f32[16,2,128,128]{2,3,1,0:T(8,128)S(1)}, f32[16,2,128,128]{2,3,1,0:T(8,128)}, u32[]{:S(2)}) copy-start(f32[16,2,128,128]{2,3,1,0:T(8,128)} %copy.41) | copy-start | bytes 6291460 | tf_op jit(solution)/shard_map/while
Sparse Core Ops, SparseCore 0:
  9.6 48.3 all-gather.2
  59.9 35.3 all-gather.4
  163.8 33.5 reduce-scatter.3
where the time goes:
time: 215 us; the launch traced here: 214 us
  waiting for transfers between devices  63.7 us (30%)
  blocking collectives  61 us (28%)
  local copies, waits for them, and re-layouts  44.8 us (21%)
  matrix products  26.4 us (12%)
  between operations  15.6 us (7%)
    psum x1, blocking collectives, on_device(): overall = lax.psum(jnp.sum(partial_value), ('row', 'col'))  39.5 us
    all_gather x1, waiting for transfers between devices, gathered(): return lax.all_gather(part, axis, axis=dim, tiled=True)  37.3 us
    all_gather x1, waiting for transfers between devices, on_device(): col_tiles = lax.all_gather(tile_data, 'row', axis=1, tiled=True)  25 us
    gather x8, local copies, waits for them, and re-layouts, tile_counts(): partner = col_tiles[clipped]  19.9 us
    dot_general x8, matrix products, tile_counts(): jnp.einsum('pxy,pqyz->pqxz', stored, partner, preferred_element_type=jnp....  14.9 us
    dot_general x8, local copies, waits for them, and re-layouts, tile_counts(): jnp.einsum('pqs,sxz->pqxz', weights, own_tiles, preferred_element_type=jn...  14.7 us
    all_gather x1, blocking collectives, on_device(): col_index = lax.all_gather(tile_cols, 'row', axis=1, tiled=True)  12.6 us
    dot_general x8, matrix products, tile_counts(): jnp.einsum('pqs,sxz->pqxz', weights, own_tiles, preferred_element_type=jn...  11.5 us
  transfers between devices with their start and end apart: 3, of which 2 were waited for; matrix products, arithmetic and copies ran while one was open for 2% of the time, Pallas kernels for 0%

commit v1 on v0

--- a/solution.py
+++ b/solution.py
@@ -29,6 +29,19 @@
 
 
 def on_device(tile_data, tile_cols):
+
+    def heaps_read(base_x):
+        axis_total = lax.axis_size("row")
+        by_rank = tuple(((to_i, (to_i + 1) % axis_total) for to_i in range(axis_total)))
+
+        def point_the_case(e_now):
+            if len(e_now) == axis_total:
+                return e_now
+            return point_the_case([lax.ppermute(e_now[0], "row", perm=by_rank), *e_now])
+
+        met_up = jnp.concatenate(point_the_case([base_x]), axis=1)
+        return jnp.roll(met_up, (lax.axis_index("row") + 1) * base_x.shape[1], axis=1)
+
     rows_here = tile_data.shape[0]
     slots = tile_data.shape[3]
     width = tile_data.shape[4]
@@ -36,7 +49,7 @@
     own_cols = tile_cols[:, 0, 0]
     row_index = lax.all_gather(tile_cols, "col", axis=2, tiled=True)
     col_index = lax.all_gather(tile_cols, "row", axis=1, tiled=True)
-    col_tiles = lax.all_gather(tile_data, "row", axis=1, tiled=True)
+    col_tiles = heaps_read(tile_data)
     tile_rows = col_index.shape[0] * col_index.shape[1]
     col_index = col_index.reshape(tile_rows, slots)
     col_tiles = col_tiles.reshape(tile_rows, slots, width, width)

time: 215 us -> 185 us (0.86)
  waiting for transfers between devices: 63.7 us -> 29.8 us
  starting transfers between devices: 0.11 us -> 3.19 us
    all_gather x1, waiting for transfers between devices: 37.3 us -> 0.01 us  [gathered(): return lax.all_gather(part, axis, axis=dim, tiled=True)]
    ppermute x0 -> x3, waiting for transfers between devices: none -> 29 us  [point_the_case(): return point_the_case([lax.ppermute(e_now[0], 'row', perm=by_rank), *e_now])]
    all_gather x1 -> x0, waiting for transfers between devices: 25 us -> none  [on_device(): col_tiles = lax.all_gather(tile_data, 'row', axis=1, tiled=True)]
    dot_general x8, matrix products: 11.5 us -> 4.81 us  [tile_counts(): jnp.einsum('pqs,sxz->pqxz', weights, own_tiles, preferred_element_type=jn...]
    dot_general x8, matrix products: 14.9 us -> 20.7 us  [tile_counts(): jnp.einsum('pxy,pqyz->pqxz', stored, partner, preferred_element_type=jnp....]
    ppermute x0 -> x3, starting transfers between devices: none -> 3.11 us  [point_the_case(): return point_the_case([lax.ppermute(e_now[0], 'row', perm=by_rank), *e_now])]
    unnamed x7 -> x14, local copies, waits for them, and re-layouts: 4.42 us -> 4.06 us
  transfers between devices with their start and end apart: 3 -> 5, of which waited for: 2 -> 2; matrix products, arithmetic and copies ran while one was open for 2% -> 3% of each run, Pallas kernels for 0% -> 0%
where the time goes in v1:
time: 185 us; the launch traced here: 184 us
  blocking collectives  62.6 us (34%)
  local copies, waits for them, and re-layouts  45.4 us (25%)
  waiting for transfers between devices  29.8 us (16%)
  matrix products  25.5 us (14%)
  between operations  16 us (9%)
  starting transfers between devices  3.19 us (2%)
    psum x1, blocking collectives, on_device(): overall = lax.psum(jnp.sum(partial_value), ('row', 'col'))  39.6 us
    ppermute x3, waiting for transfers between devices, point_the_case(): return point_the_case([lax.ppermute(e_now[0], 'row', perm=by_rank), *e_now])  29 us
    dot_general x8, matrix products, tile_counts(): jnp.einsum('pxy,pqyz->pqxz', stored, partner, preferred_element_type=jnp....  20.7 us
    gather x8, local copies, waits for them, and re-layouts, tile_counts(): partner = col_tiles[clipped]  18.7 us
    dot_general x8, local copies, waits for them, and re-layouts, tile_counts(): jnp.einsum('pqs,sxz->pqxz', weights, own_tiles, preferred_element_type=jn...  14.7 us
    all_gather x1, blocking collectives, on_device(): col_index = lax.all_gather(tile_cols, 'row', axis=1, tiled=True)  14.3 us
    all_gather x1, blocking collectives, on_device(): row_index = lax.all_gather(tile_cols, 'col', axis=2, tiled=True)  8.63 us
    gather x16, local copies, waits for them, and re-layouts, tile_counts(): partner_cols = col_index[clipped]  5.15 us
  transfers between devices with their start and end apart: 5, of which 2 were waited for; matrix products, arithmetic and copies ran while one was open for 3% of the time, Pallas kernels for 0%

profile of v1, /device:TPU:0, one launch (start us, length us, event | category | flops | bytes accessed | tf_op | source)
XLA Modules:
  0.0 184.3 jit_solution(2837086428151928363)
XLA Ops:
  7.2 0.7 all-gather.2.cloned.1.call-update
  8.0 3.1 %collective-permute-start = (bf16[8,1,1,2,128,128]{5,4,3,2,1,0:T(8,128)(2,1)}, bf16[8,1,1,2,128,128]{5,4,3,2,1,0:T(8,128)(2,1)S(1)}, u32[]{:S(2)}, u32[]{:S(2)}) collective-permute-start(bf16[8,1,1,2,128,128]{5,4,3,2,1,0:T(8,128)(2,1)} %param.4), channel_id=1, source_target_pairs={{0,8},{8,16},{16,24},{24,0},{1,9},{9,17},{17,25},{25,1},{2,10},{10... | collective-permute-start | bytes 1572872 | tf_op jit(solution)/shard_map/ppermute | solution.py:40
  11.1 14.2 %collective-permute-done = bf16[8,1,1,2,128,128]{5,4,3,2,1,0:T(8,128)(2,1)S(1)} collective-permute-done((bf16[8,1,1,2,128,128]{5,4,3,2,1,0:T(8,128)(2,1)}, bf16[8,1,1,2,128,128]{5,4,3,2,1,0:T(8,128)(2,1)S(1)}, u32[]{:S(2)}, u32[]{:S(2)}) %collective-permute-start) | collective-permute-done | bytes 524320 | tf_op jit(solution)/shard_map/ppermute | solution.py:40
  25.2 14.9 %collective-permute-done.1 = bf16[8,1,1,2,128,128]{5,4,3,2,1,0:T(8,128)(2,1)S(1)} collective-permute-done((bf16[8,1,1,2,128,128]{5,4,3,2,1,0:T(8,128)(2,1)S(1)}, bf16[8,1,1,2,128,128]{5,4,3,2,1,0:T(8,128)(2,1)S(1)}, u32[]{:S(2)}, u32[]{:S(2)}) %collective-permute-start.1) | collective-permute-done | bytes 524320 | tf_op jit(solution)/shard_map/ppermute | solution.py:40
  40.1 1.6 copy.37
  41.7 14.3 %all_gather.11 = s32[8,4,1,2]{0,3,2,1:T(2,128)S(1)} all-gather(s32[8,1,1,2]{0,3,2,1:T(2,128)} %param.5), channel_id=1, replica_groups=mesh['row'=4,'col'=8] {'row'}, dimensions={1}, use_global_device_ids=true | all-gather | bytes 320 | tf_op jit(solution)/shard_map/all_gather | solution.py:51
  56.1 8.6 %all_gather.9 = s32[8,1,8,2]{0,3,1,2:T(2,128)S(1)} all-gather(s32[8,1,1,2]{0,3,1,2:T(2,128)} %bitcast.69), channel_id=1, replica_groups=mesh['row'=4,'col'=8] {'col'}, dimensions={2}, use_global_device_ids=true | all-gather | bytes 576 | tf_op jit(solution)/shard_map/all_gather | solution.py:50
  64.8 0.8 copy.28
  66.2 1.5 constant_dynamic-slice_fusion.2
  67.7 65.1 %while.10 = (s32[]{:T(128)}, f32[8,128]{1,0:T(8,128)S(1)}, s32[8,16]{1,0:T(8,128)S(1)}, bf16[32,2,128,128]{3,2,1,0:T(8,128)(2,1)}, bf16[8,16,128,128]{3,2,1,0:T(...) while((s32[]{:T(128)}, f32[8,128]{1,0:T(8,128)S(1)}, ...), condition=%wide.region_2.3_spmd, body=%wide.region_0.2_spmd.sunk | while | flops 137364624 | bytes 12133915 | solution.py:66
  68.4 0.6 fusion.32
  69.0 1.8 %copy.41 = f32[16,2,128,128]{2,3,1,0:T(8,128)} copy(f32[16,2,128,128]{3,0,2,1:T(8,128)S(1)} %fusion.32) | data formatting | bytes 4194304 | tf_op jit(solution)/shard_map/while/body/eval_jaxpr/pqs,sxz->pqxz/dot_general | solution.py:26
  70.8 2.3 %gather_fusion.1 = bf16[16,2,128,128]{3,2,1,0:T(8,128)(2,1)S(1)} fusion(bf16[32,2,128,128]{3,2,1,0:T(8,128)(2,1)} %get-tuple-element.163, s32[1024]{0:T(1024)S(1)} %pad_clamp_fusion.2), kind=kCustom, calls=%fused_computation.clone.1 | custom fusion | bytes 2097216 | tf_op jit(solution)/shard_map/while/body/eval_jaxpr/gather | solution.py:21
  73.2 2.6 %fusion.33 = f32[128]{0:T(128)S(1)} fusion(f32[16,2,128,128]{2,3,1,0:T(8,128)} %copy.41, bf16[16,2,128,128]{3,2,1,0:T(8,128)(2,1)S(1)} %gather_fusion.1, bf16[8,16,128,128]{3,2,1,0:T(8,128)(2,1)} %get-tuple-element.164, s32[]{:T(128)} %get-tuple-element.150), kind=kOutput, calls=%fused_computation.3.clone.1 | convolution fusion | flops 135266176 | bytes 3671040 | tf_op jit(solution)/shard_map/while/body/eval_jaxpr/pxy,pqyz->pqxz/dot_general | solution.py:27
  76.5 0.6 fusion.32
  77.1 1.8 %copy.41 = f32[16,2,128,128]{2,3,1,0:T(8,128)} copy(f32[16,2,128,128]{3,0,2,1:T(8,128)S(1)} %fusion.32) | data formatting | bytes 4194304 | tf_op jit(solution)/shard_map/while/body/eval_jaxpr/pqs,sxz->pqxz/dot_general | solution.py:26
  79.0 2.3 %gather_fusion.1 = bf16[16,2,128,128]{3,2,1,0:T(8,128)(2,1)S(1)} fusion(bf16[32,2,128,128]{3,2,1,0:T(8,128)(2,1)} %get-tuple-element.163, s32[1024]{0:T(1024)S(1)} %pad_clamp_fusion.2), kind=kCustom, calls=%fused_computation.clone.1 | custom fusion | bytes 2097216 | tf_op jit(solution)/shard_map/while/body/eval_jaxpr/gather | solution.py:21
  81.3 2.6 %fusion.33 = f32[128]{0:T(128)S(1)} fusion(f32[16,2,128,128]{2,3,1,0:T(8,128)} %copy.41, bf16[16,2,128,128]{3,2,1,0:T(8,128)(2,1)S(1)} %gather_fusion.1, bf16[8,16,128,128]{3,2,1,0:T(8,128)(2,1)} %get-tuple-element.164, s32[]{:T(128)} %get-tuple-element.150), kind=kOutput, calls=%fused_computation.3.clone.1 | convolution fusion | flops 135266176 | bytes 3671040 | tf_op jit(solution)/shard_map/while/body/eval_jaxpr/pxy,pqyz->pqxz/dot_general | solution.py:27
  84.6 0.6 fusion.32
  85.2 1.8 %copy.41 = f32[16,2,128,128]{2,3,1,0:T(8,128)} copy(f32[16,2,128,128]{3,0,2,1:T(8,128)S(1)} %fusion.32) | data formatting | bytes 4194304 | tf_op jit(solution)/shard_map/while/body/eval_jaxpr/pqs,sxz->pqxz/dot_general | solution.py:26
  87.1 2.3 %gather_fusion.1 = bf16[16,2,128,128]{3,2,1,0:T(8,128)(2,1)S(1)} fusion(bf16[32,2,128,128]{3,2,1,0:T(8,128)(2,1)} %get-tuple-element.163, s32[1024]{0:T(1024)S(1)} %pad_clamp_fusion.2), kind=kCustom, calls=%fused_computation.clone.1 | custom fusion | bytes 2097216 | tf_op jit(solution)/shard_map/while/body/eval_jaxpr/gather | solution.py:21
  89.4 2.6 %fusion.33 = f32[128]{0:T(128)S(1)} fusion(f32[16,2,128,128]{2,3,1,0:T(8,128)} %copy.41, bf16[16,2,128,128]{3,2,1,0:T(8,128)(2,1)S(1)} %gather_fusion.1, bf16[8,16,128,128]{3,2,1,0:T(8,128)(2,1)} %get-tuple-element.164, s32[]{:T(128)} %get-tuple-element.150), kind=kOutput, calls=%fused_computation.3.clone.1 | convolution fusion | flops 135266176 | bytes 3671040 | tf_op jit(solution)/shard_map/while/body/eval_jaxpr/pxy,pqyz->pqxz/dot_general | solution.py:27
  92.1 0.6 gather_fusion
  92.8 0.6 fusion.32
  93.4 1.8 %copy.41 = f32[16,2,128,128]{2,3,1,0:T(8,128)} copy(f32[16,2,128,128]{3,0,2,1:T(8,128)S(1)} %fusion.32) | data formatting | bytes 4194304 | tf_op jit(solution)/shard_map/while/body/eval_jaxpr/pqs,sxz->pqxz/dot_general | solution.py:26
  95.2 2.3 %gather_fusion.1 = bf16[16,2,128,128]{3,2,1,0:T(8,128)(2,1)S(1)} fusion(bf16[32,2,128,128]{3,2,1,0:T(8,128)(2,1)} %get-tuple-element.163, s32[1024]{0:T(1024)S(1)} %pad_clamp_fusion.2), kind=kCustom, calls=%fused_computation.clone.1 | custom fusion | bytes 2097216 | tf_op jit(solution)/shard_map/while/body/eval_jaxpr/gather | solution.py:21
  97.6 2.6 %fusion.33 = f32[128]{0:T(128)S(1)} fusion(f32[16,2,128,128]{2,3,1,0:T(8,128)} %copy.41, bf16[16,2,128,128]{3,2,1,0:T(8,128)(2,1)S(1)} %gather_fusion.1, bf16[8,16,128,128]{3,2,1,0:T(8,128)(2,1)} %get-tuple-element.164, s32[]{:T(128)} %get-tuple-element.150), kind=kOutput, calls=%fused_computation.3.clone.1 | convolution fusion | flops 135266176 | bytes 3671040 | tf_op jit(solution)/shard_map/while/body/eval_jaxpr/pxy,pqyz->pqxz/dot_general | solution.py:27
  100.9 0.6 fusion.32
  101.5 1.8 %copy.41 = f32[16,2,128,128]{2,3,1,0:T(8,128)} copy(f32[16,2,128,128]{3,0,2,1:T(8,128)S(1)} %fusion.32) | data formatting | bytes 4194304 | tf_op jit(solution)/shard_map/while/body/eval_jaxpr/pqs,sxz->pqxz/dot_general | solution.py:26
  103.4 2.3 %gather_fusion.1 = bf16[16,2,128,128]{3,2,1,0:T(8,128)(2,1)S(1)} fusion(bf16[32,2,128,128]{3,2,1,0:T(8,128)(2,1)} %get-tuple-element.163, s32[1024]{0:T(1024)S(1)} %pad_clamp_fusion.2), kind=kCustom, calls=%fused_computation.clone.1 | custom fusion | bytes 2097216 | tf_op jit(solution)/shard_map/while/body/eval_jaxpr/gather | solution.py:21
  105.7 2.6 %fusion.33 = f32[128]{0:T(128)S(1)} fusion(f32[16,2,128,128]{2,3,1,0:T(8,128)} %copy.41, bf16[16,2,128,128]{3,2,1,0:T(8,128)(2,1)S(1)} %gather_fusion.1, bf16[8,16,128,128]{3,2,1,0:T(8,128)(2,1)} %get-tuple-element.164, s32[]{:T(128)} %get-tuple-element.150), kind=kOutput, calls=%fused_computation.3.clone.1 | convolution fusion | flops 135266176 | bytes 3671040 | tf_op jit(solution)/shard_map/while/body/eval_jaxpr/pxy,pqyz->pqxz/dot_general | solution.py:27
  109.0 0.6 fusion.32
  109.7 1.8 %copy.41 = f32[16,2,128,128]{2,3,1,0:T(8,128)} copy(f32[16,2,128,128]{3,0,2,1:T(8,128)S(1)} %fusion.32) | data formatting | bytes 4194304 | tf_op jit(solution)/shard_map/while/body/eval_jaxpr/pqs,sxz->pqxz/dot_general | solution.py:26
  111.5 2.3 %gather_fusion.1 = bf16[16,2,128,128]{3,2,1,0:T(8,128)(2,1)S(1)} fusion(bf16[32,2,128,128]{3,2,1,0:T(8,128)(2,1)} %get-tuple-element.163, s32[1024]{0:T(1024)S(1)} %pad_clamp_fusion.2), kind=kCustom, calls=%fused_computation.clone.1 | custom fusion | bytes 2097216 | tf_op jit(solution)/shard_map/while/body/eval_jaxpr/gather | solution.py:21
  113.8 2.6 %fusion.33 = f32[128]{0:T(128)S(1)} fusion(f32[16,2,128,128]{2,3,1,0:T(8,128)} %copy.41, bf16[16,2,128,128]{3,2,1,0:T(8,128)(2,1)S(1)} %gather_fusion.1, bf16[8,16,128,128]{3,2,1,0:T(8,128)(2,1)} %get-tuple-element.164, s32[]{:T(128)} %get-tuple-element.150), kind=kOutput, calls=%fused_computation.3.clone.1 | convolution fusion | flops 135266176 | bytes 3671040 | tf_op jit(solution)/shard_map/while/body/eval_jaxpr/pxy,pqyz->pqxz/dot_general | solution.py:27
  117.2 0.6 fusion.32
  117.8 1.8 %copy.41 = f32[16,2,128,128]{2,3,1,0:T(8,128)} copy(f32[16,2,128,128]{3,0,2,1:T(8,128)S(1)} %fusion.32) | data formatting | bytes 4194304 | tf_op jit(solution)/shard_map/while/body/eval_jaxpr/pqs,sxz->pqxz/dot_general | solution.py:26
  119.6 2.3 %gather_fusion.1 = bf16[16,2,128,128]{3,2,1,0:T(8,128)(2,1)S(1)} fusion(bf16[32,2,128,128]{3,2,1,0:T(8,128)(2,1)} %get-tuple-element.163, s32[1024]{0:T(1024)S(1)} %pad_clamp_fusion.2), kind=kCustom, calls=%fused_computation.clone.1 | custom fusion | bytes 2097216 | tf_op jit(solution)/shard_map/while/body/eval_jaxpr/gather | solution.py:21
  122.0 2.6 %fusion.33 = f32[128]{0:T(128)S(1)} fusion(f32[16,2,128,128]{2,3,1,0:T(8,128)} %copy.41, bf16[16,2,128,128]{3,2,1,0:T(8,128)(2,1)S(1)} %gather_fusion.1, bf16[8,16,128,128]{3,2,1,0:T(8,128)(2,1)} %get-tuple-element.164, s32[]{:T(128)} %get-tuple-element.150), kind=kOutput, calls=%fused_computation.3.clone.1 | convolution fusion | flops 135266176 | bytes 3671040 | tf_op jit(solution)/shard_map/while/body/eval_jaxpr/pxy,pqyz->pqxz/dot_general | solution.py:27
  125.3 0.6 fusion.32
  125.9 1.8 %copy.41 = f32[16,2,128,128]{2,3,1,0:T(8,128)} copy(f32[16,2,128,128]{3,0,2,1:T(8,128)S(1)} %fusion.32) | data formatting | bytes 4194304 | tf_op jit(solution)/shard_map/while/body/eval_jaxpr/pqs,sxz->pqxz/dot_general | solution.py:26
  127.8 2.3 %gather_fusion.1 = bf16[16,2,128,128]{3,2,1,0:T(8,128)(2,1)S(1)} fusion(bf16[32,2,128,128]{3,2,1,0:T(8,128)(2,1)} %get-tuple-element.163, s32[1024]{0:T(1024)S(1)} %pad_clamp_fusion.2), kind=kCustom, calls=%fused_computation.clone.1 | custom fusion | bytes 2097216 | tf_op jit(solution)/shard_map/while/body/eval_jaxpr/gather | solution.py:21
  130.1 2.6 %fusion.33 = f32[128]{0:T(128)S(1)} fusion(f32[16,2,128,128]{2,3,1,0:T(8,128)} %copy.41, bf16[16,2,128,128]{3,2,1,0:T(8,128)(2,1)S(1)} %gather_fusion.1, bf16[8,16,128,128]{3,2,1,0:T(8,128)(2,1)} %get-tuple-element.164, s32[]{:T(128)} %get-tuple-element.150), kind=kOutput, calls=%fused_computation.3.clone.1 | convolution fusion | flops 135266176 | bytes 3671040 | tf_op jit(solution)/shard_map/while/body/eval_jaxpr/pxy,pqyz->pqxz/dot_general | solution.py:27
  133.0 0.8 bitcast_reduce_fusion
  133.9 0.6 reduce_sum.18
  134.5 39.6 %psum.7 = f32[]{:T(128)} all-reduce(f32[]{:T(128)} %reduce_sum.18), channel_id=1, replica_groups=mesh['row'=4,'col'=8] {'row','col'}, use_global_device_ids=true, to_apply=%region_5.6 | all-reduce | flops 1 | bytes 8 | tf_op jit(solution)/shard_map/psum | solution.py:74
  174.8 0.8 reshape_bitcast_fusion
  175.7 0.6 broadcast_multiply_fusion
  (78 shorter events, 6.4 us)
Async XLA Ops:
  7.2 58.6 %copy-start = (bf16[8,1,1,2,128,128]{5,4,3,2,1,0:T(8,128)(2,1)S(1)}, bf16[8,1,1,2,128,128]{5,4,3,2,1,0:T(8,128)(2,1)}, u32[]{:S(2)}) copy-start(bf16[8,1,1,2,128,128]{5,4,3,2,1,0:T(8,128)(2,1)} %param.4) | copy-start | bytes 1572868
  7.2 60.5 %all-gather.2.cloned.1.call-start = ((), (), s32[]{:S(2)}) async-start(), calls=%async_computation.1 | async-start | bytes 4718592 | tf_op jit(solution)/shard_map/all_gather | solution.py:13
  7.9 166.9 %reduce-scatter.4.cloned.1.call-start = ((), (), s32[]{:S(2)}) async-start(), calls=%async_computation.2 | async-start | bytes 73728
  8.0 17.3 %collective-permute-start = (bf16[8,1,1,2,128,128]{5,4,3,2,1,0:T(8,128)(2,1)}, bf16[8,1,1,2,128,128]{5,4,3,2,1,0:T(8,128)(2,1)S(1)}, u32[]{:S(2)}, u32[]{:S(2)}) collective-permute-start(bf16[8,1,1,2,128,128]{5,4,3,2,1,0:T(8,128)(2,1)} %param.4), channel_id=1, source_target_pairs={{0,8},{8,16},{16,24},{24,0},{1,9},{9,17},{17,25},{25,1},{2,10},{10... | collective-permute-start | bytes 1572872 | tf_op jit(solution)/shard_map/ppermute | solution.py:40
  25.2 14.9 %collective-permute-start.1 = (bf16[8,1,1,2,128,128]{5,4,3,2,1,0:T(8,128)(2,1)S(1)}, bf16[8,1,1,2,128,128]{5,4,3,2,1,0:T(8,128)(2,1)S(1)}, u32[]{:S(2)}, u32[]{:S(2)}) collective-permute-start(bf16[8,1,1,2,128,128]{5,4,3,2,1,0:T(8,128)(2,1)S(1)} %collective-permute-done), channel_id=1, source_target_pairs={{0,8},{8,16},{16,24},{24,0},{1,9},{9,17},{17,25},{25,1},{2,10},{10... | collective-permute-start | bytes 1572872 | tf_op jit(solution)/shard_map/ppermute | solution.py:40
  40.1 25.5 %collective-permute-start.2 = (bf16[8,1,1,2,128,128]{5,4,3,2,1,0:T(8,128)(2,1)S(1)}, bf16[8,1,1,2,128,128]{5,4,3,2,1,0:T(8,128)(2,1)S(1)}, u32[]{:S(2)}, u32[]{:S(2)}) collective-permute-start(bf16[8,1,1,2,128,128]{5,4,3,2,1,0:T(8,128)(2,1)S(1)} %collective-permute-done.1), channel_id=1, source_target_pairs={{0,8},{8,16},{16,24},{24,0},{1,9},{9,17},{17,25},{25,1},{2,10},{10... | collective-permute-start | bytes 1572872 | tf_op jit(solution)/shard_map/ppermute | solution.py:40
Sparse Core Ops, SparseCore 0:
  9.9 39.2 all-gather.1
  134.0 31.8 reduce-scatter.3
